TPU v7x, 32 devices: a whole 2x2x4 slice. The times are simulated.
32 devices in a mesh: tok: 8 (over z, y), vocab: 4 (over x, core).
Axes of the slice: x: 2, y: 2, z: 4, core: 2. Of those that a mesh axis runs over, the one named last changes fastest.
Arguments:
- hidden: bfloat16 [192, 9216], P('tok'), may hold values from -256 to 256
- policy_head: bfloat16 [9216, 32768], P(None, ('tok', 'vocab')), may hold values from -0.0625 to 0.0625
- reference_head: bfloat16 [9216, 32768], P(None, ('tok', 'vocab')), may hold values from -0.0625 to 0.0625
- targets: int32 [192], P('tok'), may hold values from 0 to 32767
Outputs:
- policy_logprob: float32 [192], P('tok')
- reference_logprob: float32 [192], P('tok')
- divergence: float32 [192], P('tok')
All inputs are finite; a program needn't handle non-finite values.
Results may differ from a plain program's by a relative error of at most 0.00055.
Values may be sent and summed in bfloat16 or wider, within the bound.
A program may use at most 128 MiB of HBM per device.

v0:
```python
import jax
import jax.numpy as jnp
from jax import lax
from jax.sharding import PartitionSpec as P


def combined_all(value, axis, combine):
    everything = jax.tree.map(lambda part: lax.all_gather(part, axis), value)
    leading = jax.tree.map(lambda part: part[0], everything)

    def step(k, so_far):
        return combine(so_far, jax.tree.map(lambda part: part[k], everything))

    return lax.fori_loop(1, lax.axis_size(axis), step, leading)


def local_sums(policy_logits, reference_logits, target_hits, peak_policy, peak_reference):
    policy_exp = jnp.exp(policy_logits - peak_policy[:, None])
    reference_exp = jnp.exp(reference_logits - peak_reference[:, None])
    total_policy = jnp.sum(policy_exp, axis=1)
    total_reference = jnp.sum(reference_exp, axis=1)
    weighted = jnp.sum(policy_exp * (policy_logits - reference_logits), axis=1)
    target_policy = jnp.sum(jnp.where(target_hits, policy_logits, 0.0), axis=1)
    target_reference = jnp.sum(jnp.where(target_hits, reference_logits, 0.0), axis=1)
    return (total_policy, total_reference, weighted, target_policy, target_reference)


def local_stats(policy_logits, reference_logits, target_hits):
    peak_policy = jnp.max(policy_logits, axis=1)
    peak_reference = jnp.max(reference_logits, axis=1)
    summed = local_sums(policy_logits, reference_logits, target_hits, peak_policy, peak_reference)
    return (peak_policy, peak_reference) + summed


def combine_stats(left_stats, right_stats):
    peak_policy = jnp.maximum(left_stats[0], right_stats[0])
    peak_reference = jnp.maximum(left_stats[1], right_stats[1])
    left_policy = jnp.exp(left_stats[0] - peak_policy)
    right_policy = jnp.exp(right_stats[0] - peak_policy)
    left_reference = jnp.exp(left_stats[1] - peak_reference)
    right_reference = jnp.exp(right_stats[1] - peak_reference)
    return (
        peak_policy,
        peak_reference,
        left_stats[2] * left_policy + right_stats[2] * right_policy,
        left_stats[3] * left_reference + right_stats[3] * right_reference,
        left_stats[4] * left_policy + right_stats[4] * right_policy,
        left_stats[5] + right_stats[5],
        left_stats[6] + right_stats[6],
    )


def combine_senders(received):
    peak_policy = jnp.max(received[0], axis=0)
    peak_reference = jnp.max(received[1], axis=0)
    policy_scale = jnp.exp(received[0] - peak_policy[None, :])
    reference_scale = jnp.exp(received[1] - peak_reference[None, :])
    return (
        peak_policy,
        peak_reference,
        jnp.sum(received[2] * policy_scale, axis=0),
        jnp.sum(received[3] * reference_scale, axis=0),
        jnp.sum(received[4] * policy_scale, axis=0),
        jnp.sum(received[5], axis=0),
        jnp.sum(received[6], axis=0),
    )


def finish(merged_stats):
    log_norm_policy = merged_stats[0] + jnp.log(merged_stats[2])
    log_norm_reference = merged_stats[1] + jnp.log(merged_stats[3])
    policy_logprob = merged_stats[5] - log_norm_policy
    reference_logprob = merged_stats[6] - log_norm_reference
    divergence = merged_stats[4] / merged_stats[2] - log_norm_policy + log_norm_reference
    return (policy_logprob, reference_logprob, divergence)


def body(hidden, policy_head, reference_head, targets):
    tok_count = lax.axis_size("tok")
    vocab_count = lax.axis_size("vocab")
    tok_rows = hidden.shape[0]
    vocab_cols = policy_head.shape[1]
    piece = lax.all_gather(hidden, "tok", axis=0, tiled=True)
    summed = jnp.concatenate(
        [
            jnp.dot(piece, policy_head, preferred_element_type=jnp.float32),
            jnp.dot(piece, reference_head, preferred_element_type=jnp.float32),
        ],
        axis=1,
    )
    policy_logits = summed[:, :vocab_cols]
    reference_logits = summed[:, vocab_cols:]
    every_target = lax.all_gather(targets, "tok", axis=0, tiled=True)
    block_index = lax.axis_index("tok") * vocab_count + lax.axis_index("vocab")
    vocab_ids = block_index * vocab_cols + lax.iota(jnp.int32, vocab_cols)
    target_hits = vocab_ids[None, :] == every_target[:, None]
    partial_value = local_stats(policy_logits, reference_logits, target_hits)
    shaped = tuple((entry.reshape(tok_count, tok_rows) for entry in partial_value))
    received = lax.all_to_all(shaped, "tok", split_axis=0, concat_axis=0, tiled=True)
    own_stats = combine_senders(received)
    merged_stats = combined_all(own_stats, "vocab", combine_stats)
    return finish(merged_stats)


def solution(mesh):
    in_specs = (P("tok", None), P(None, ("tok", "vocab")), P(None, ("tok", "vocab")), P("tok"))
    out_specs = (P("tok"), P("tok"), P("tok"))
    return jax.shard_map(body, mesh=mesh, in_specs=in_specs, out_specs=out_specs, check_vma=False)
```

profile of v0, /device:TPU:0, one launch (start us, length us, event | category | flops | bytes accessed | tf_op | source)
XLA Modules:
  0.0 179.8 jit_solution(15287167651976823062)
XLA Ops:
  7.2 0.0 all-gather.9.cloned.1.call-start
  7.2 0.7 all-gather.9.cloned.1.call-update
  7.9 1.2 dynamic-slice.5
  9.8 0.9 dynamic-update-slice.5
  10.7 13.1 %all-reduce.5 = s32[192]{0:T(256)S(1)} all-reduce(s32[192]{0:T(256)S(1)} %dynamic-update-slice.5), channel_id=1, replica_groups=mesh['tok'=8,'vocab'=4] {'tok'}, use_global_device_ids=true, to_apply=%add.5 | all-reduce | flops 192 | bytes 1536
  23.8 53.8 %all-gather.9.cloned.1.call-done = bf16[192,9216]{1,0:T(8,128)(2,1)} async-done(((bf16[24,9216]{1,0:T(8,128)(2,1)}), bf16[192,9216]{1,0:T(8,128)(2,1)}) %all-gather.9.cloned.1.call-update) | async-done | bytes 3538960 | tf_op jit(solution)/shard_map/all_gather | solution.py:83
  77.5 0.0 copy-start
  77.5 9.6 %fusion.24 = (f32[192]{0:T(256)S(1)}, f32[192,1024]{1,0:T(8,128)S(1)}) fusion(bf16[192,9216]{1,0:T(8,128)(2,1)} %all-gather.9.cloned.1.call-done, bf16[9216,1024]{1,0:T(8,128)(2,1)} %param.7), kind=kOutput, calls=%fused_computation.44 | convolution fusion | flops 3624075008 | bytes 23200512 | tf_op jit(solution)/shard_map/dot_general | solution.py:86
  87.2 3.1 %copy-done = bf16[9216,1024]{1,0:T(8,128)(2,1)S(1)} copy-done((bf16[9216,1024]{1,0:T(8,128)(2,1)S(1)}, bf16[9216,1024]{1,0:T(8,128)(2,1)}, u32[]{:S(2)}) %copy-start) | copy-done | bytes 18874392
  90.3 0.0 copy-start.1
  90.3 5.9 %fusion.25 = (f32[192]{0:T(256)S(1)}, f32[192,1024]{1,0:T(8,128)S(1)}) fusion(bf16[192,9216]{1,0:T(8,128)(2,1)} %all-gather.9.cloned.1.call-done, bf16[9216,1024]{1,0:T(8,128)(2,1)S(1)} %copy-done), kind=kOutput, calls=%fused_computation.45 | convolution fusion | flops 3624075008 | bytes 23200512 | tf_op jit(solution)/shard_map/dot_general | solution.py:87
  96.2 0.7 multiply_reduce_fusion
  96.9 0.7 all_to_all.64
  97.5 3.3 %all-to-all-start.4 = ((f32[8,1,24]{2,1,0:T(1,128)}), f32[8,1,24]{2,1,0:T(1,128)S(1)}, u32[]{:S(2)}, u32[]{:S(2)}) async-start(f32[8,1,24]{2,1,0:T(1,128)} %all_to_all.64), calls=%async_computation.4 | async-start | bytes 8192 | tf_op jit(solution)/shard_map/all_to_all | solution.py:99
  100.9 0.7 all_to_all.56
  101.6 5.8 %all-to-all-done.4 = f32[8,1,24]{2,1,0:T(1,128)S(1)} async-done(((f32[8,1,24]{2,1,0:T(1,128)}), f32[8,1,24]{2,1,0:T(1,128)S(1)}, u32[]{:S(2)}, u32[]{:S(2)}) %all-to-all-start.4) | async-done | bytes 800 | tf_op jit(solution)/shard_map/all_to_all | solution.py:99
  107.4 3.2 %all-to-all-start.2 = ((f32[8,1,24]{2,1,0:T(1,128)}), f32[8,1,24]{2,1,0:T(1,128)S(1)}, u32[]{:S(2)}, u32[]{:S(2)}) async-start(f32[8,1,24]{2,1,0:T(1,128)} %all_to_all.56), calls=%async_computation.2 | async-start | bytes 8192 | tf_op jit(solution)/shard_map/all_to_all | solution.py:99
  110.6 0.7 all_to_all.52
  111.3 5.7 %all-to-all-done.2 = f32[8,1,24]{2,1,0:T(1,128)S(1)} async-done(((f32[8,1,24]{2,1,0:T(1,128)}), f32[8,1,24]{2,1,0:T(1,128)S(1)}, u32[]{:S(2)}, u32[]{:S(2)}) %all-to-all-start.2) | async-done | bytes 800 | tf_op jit(solution)/shard_map/all_to_all | solution.py:99
  117.1 3.3 %all-to-all-start = ((f32[8,1,24]{2,1,0:T(1,128)}), f32[8,1,24]{2,1,0:T(1,128)S(1)}, u32[]{:S(2)}, u32[]{:S(2)}) async-start(f32[8,1,24]{2,1,0:T(1,128)} %all_to_all.52), calls=%async_computation | async-start | bytes 8192 | tf_op jit(solution)/shard_map/all_to_all | solution.py:99
  120.4 0.7 all_to_all.60
  121.1 5.8 %all-to-all-done = f32[8,1,24]{2,1,0:T(1,128)S(1)} async-done(((f32[8,1,24]{2,1,0:T(1,128)}), f32[8,1,24]{2,1,0:T(1,128)S(1)}, u32[]{:S(2)}, u32[]{:S(2)}) %all-to-all-start) | async-done | bytes 800 | tf_op jit(solution)/shard_map/all_to_all | solution.py:99
  126.8 3.2 %all-to-all-start.3 = ((f32[8,1,24]{2,1,0:T(1,128)}), f32[8,1,24]{2,1,0:T(1,128)S(1)}, u32[]{:S(2)}, u32[]{:S(2)}) async-start(f32[8,1,24]{2,1,0:T(1,128)} %all_to_all.60), calls=%async_computation.3 | async-start | bytes 8192 | tf_op jit(solution)/shard_map/all_to_all | solution.py:99
  130.1 0.7 all_to_all.54
  130.8 5.7 %all-to-all-done.3 = f32[8,1,24]{2,1,0:T(1,128)S(1)} async-done(((f32[8,1,24]{2,1,0:T(1,128)}), f32[8,1,24]{2,1,0:T(1,128)S(1)}, u32[]{:S(2)}, u32[]{:S(2)}) %all-to-all-start.3) | async-done | bytes 800 | tf_op jit(solution)/shard_map/all_to_all | solution.py:99
  136.5 3.3 %all-to-all-start.1 = ((f32[8,1,24]{2,1,0:T(1,128)}), f32[8,1,24]{2,1,0:T(1,128)S(1)}, u32[]{:S(2)}, u32[]{:S(2)}) async-start(f32[8,1,24]{2,1,0:T(1,128)} %all_to_all.54), calls=%async_computation.1 | async-start | bytes 8192 | tf_op jit(solution)/shard_map/all_to_all | solution.py:99
  139.9 0.0 copy-done.1
  139.9 0.6 dynamic-slice
  141.1 0.7 all_to_all.67
  141.8 0.7 all_to_all.69
  142.5 3.8 %all-to-all-done.1 = f32[8,1,24]{2,1,0:T(1,128)S(1)} async-done(((f32[8,1,24]{2,1,0:T(1,128)}), f32[8,1,24]{2,1,0:T(1,128)S(1)}, u32[]{:S(2)}, u32[]{:S(2)}) %all-to-all-start.1) | async-done | bytes 800 | tf_op jit(solution)/shard_map/all_to_all | solution.py:99
  146.3 3.2 %all-to-all-start.5 = ((f32[8,1,24]{2,1,0:T(1,128)}), f32[8,1,24]{2,1,0:T(1,128)S(1)}, u32[]{:S(2)}, u32[]{:S(2)}) async-start(f32[8,1,24]{2,1,0:T(1,128)} %all_to_all.67), calls=%async_computation.5 | async-start | bytes 8192 | tf_op jit(solution)/shard_map/all_to_all | solution.py:99
  149.6 6.4 %all-to-all-done.5 = f32[8,1,24]{2,1,0:T(1,128)S(1)} async-done(((f32[8,1,24]{2,1,0:T(1,128)}), f32[8,1,24]{2,1,0:T(1,128)S(1)}, u32[]{:S(2)}, u32[]{:S(2)}) %all-to-all-start.5) | async-done | bytes 800 | tf_op jit(solution)/shard_map/all_to_all | solution.py:99
  156.0 3.3 %all-to-all-start.6 = ((f32[8,1,24]{2,1,0:T(1,128)}), f32[8,1,24]{2,1,0:T(1,128)S(1)}, u32[]{:S(2)}, u32[]{:S(2)}) async-start(f32[8,1,24]{2,1,0:T(1,128)} %all_to_all.69), calls=%async_computation.6 | async-start | bytes 8192 | tf_op jit(solution)/shard_map/all_to_all | solution.py:99
  159.3 0.2 dynamic-update-slice
  159.5 0.2 dynamic-update-slice.1
  159.7 0.2 dynamic-update-slice.4
  159.9 0.2 dynamic-update-slice.2
  160.1 0.2 dynamic-update-slice.3
  160.4 0.2 dynamic-update-slice.6
  160.6 5.1 %all-to-all-done.6 = f32[8,1,24]{2,1,0:T(1,128)S(1)} async-done(((f32[8,1,24]{2,1,0:T(1,128)}), f32[8,1,24]{2,1,0:T(1,128)S(1)}, u32[]{:S(2)}, u32[]{:S(2)}) %all-to-all-start.6) | async-done | bytes 800 | tf_op jit(solution)/shard_map/all_to_all | solution.py:99
  165.7 0.2 dynamic-update-slice.7
  165.9 5.6 %all-reduce.8 = (f32[96]{0:T(128)S(1)}, f32[96]{0:T(128)S(1)}, f32[96]{0:T(128)S(1)}, f32[96]{0:T(128)S(1)}, f32[96]{0:T(128)S(1)}, /*index=5*/f32[96]{0:T(128)S(1)}, f32[96]{0:T(128)S(1)}) all-reduce(f32[96]{0:T(128)S(1)} %dynamic-update-slice, f32[96]{0:T(128)S(1)} %dynamic-update-slice.1, ...), channel_id=2, replica_groups=mesh['tok'=8,'vocab'=4] {'vocab'}, use_global_device_ids=true, to_apply=%add | all-reduce | flops 672 | bytes 5376
  171.6 0.1 reshape.43
  171.7 0.1 reshape.44
  171.7 0.1 reshape.45
  171.8 0.1 reshape.46
  171.9 0.1 reshape.47
  172.0 0.1 reshape.48
  172.1 0.1 reshape.49
  172.2 0.3 while.27
  172.5 0.5 subtract_add_fusion
  (27 shorter events, 0.4 us)
Async XLA Ops:
  7.2 70.3 %all-gather.9.cloned.1.call-start = ((), (), s32[]{:S(2)}) async-start(), calls=%async_computation.7 | async-start | bytes 3981312 | tf_op jit(solution)/shard_map/all_gather | solution.py:83
  77.5 12.7 %copy-start = (bf16[9216,1024]{1,0:T(8,128)(2,1)S(1)}, bf16[9216,1024]{1,0:T(8,128)(2,1)}, u32[]{:S(2)}) copy-start(bf16[9216,1024]{1,0:T(8,128)(2,1)} %param.8) | copy-start | bytes 56623108
  90.3 49.6 %copy-start.1 = (u32[32]{0:T(128)S(1)}, u32[32]{0:T(128)}, u32[]{:S(2)}) copy-start(u32[32]{0:T(128)} %constant.57) | copy-start | bytes 388
  97.5 9.8 %all-to-all-start.4 = ((f32[8,1,24]{2,1,0:T(1,128)}), f32[8,1,24]{2,1,0:T(1,128)S(1)}, u32[]{:S(2)}, u32[]{:S(2)}) async-start(f32[8,1,24]{2,1,0:T(1,128)} %all_to_all.64), calls=%async_computation.4 | async-start | bytes 8192 | tf_op jit(solution)/shard_map/all_to_all | solution.py:99
  107.4 9.7 %all-to-all-start.2 = ((f32[8,1,24]{2,1,0:T(1,128)}), f32[8,1,24]{2,1,0:T(1,128)S(1)}, u32[]{:S(2)}, u32[]{:S(2)}) async-start(f32[8,1,24]{2,1,0:T(1,128)} %all_to_all.56), calls=%async_computation.2 | async-start | bytes 8192 | tf_op jit(solution)/shard_map/all_to_all | solution.py:99
  117.1 9.8 %all-to-all-start = ((f32[8,1,24]{2,1,0:T(1,128)}), f32[8,1,24]{2,1,0:T(1,128)S(1)}, u32[]{:S(2)}, u32[]{:S(2)}) async-start(f32[8,1,24]{2,1,0:T(1,128)} %all_to_all.52), calls=%async_computation | async-start | bytes 8192 | tf_op jit(solution)/shard_map/all_to_all | solution.py:99
  126.8 9.7 %all-to-all-start.3 = ((f32[8,1,24]{2,1,0:T(1,128)}), f32[8,1,24]{2,1,0:T(1,128)S(1)}, u32[]{:S(2)}, u32[]{:S(2)}) async-start(f32[8,1,24]{2,1,0:T(1,128)} %all_to_all.60), calls=%async_computation.3 | async-start | bytes 8192 | tf_op jit(solution)/shard_map/all_to_all | solution.py:99
  136.5 9.8 %all-to-all-start.1 = ((f32[8,1,24]{2,1,0:T(1,128)}), f32[8,1,24]{2,1,0:T(1,128)S(1)}, u32[]{:S(2)}, u32[]{:S(2)}) async-start(f32[8,1,24]{2,1,0:T(1,128)} %all_to_all.54), calls=%async_computation.1 | async-start | bytes 8192 | tf_op jit(solution)/shard_map/all_to_all | solution.py:99
  146.3 9.7 %all-to-all-start.5 = ((f32[8,1,24]{2,1,0:T(1,128)}), f32[8,1,24]{2,1,0:T(1,128)S(1)}, u32[]{:S(2)}, u32[]{:S(2)}) async-start(f32[8,1,24]{2,1,0:T(1,128)} %all_to_all.67), calls=%async_computation.5 | async-start | bytes 8192 | tf_op jit(solution)/shard_map/all_to_all | solution.py:99
  156.0 9.7 %all-to-all-start.6 = ((f32[8,1,24]{2,1,0:T(1,128)}), f32[8,1,24]{2,1,0:T(1,128)S(1)}, u32[]{:S(2)}, u32[]{:S(2)}) async-start(f32[8,1,24]{2,1,0:T(1,128)} %all_to_all.69), calls=%async_computation.6 | async-start | bytes 8192 | tf_op jit(solution)/shard_map/all_to_all | solution.py:99
Sparse Core Ops, SparseCore 0:
  10.2 67.3 all-gather.8
where the time goes:
time: 180 us
  waiting for transfers between devices  92.7 us (52%)
  starting transfers between devices  23.1 us (13%)
  blocking collectives  18.7 us (10%)
  matrix products  15.6 us (9%)
  between operations  15.5 us (9%)
  local copies, waits for them, and re-layouts  12.7 us (7%)
    all_gather x1, waiting for transfers between devices, body(): piece = lax.all_gather(hidden, 'tok', axis=0, tiled=True)  53.8 us
    all_to_all x7, waiting for transfers between devices, body(): lax.all_to_all(shaped, 'tok', split_axis=0, concat_axis=0, tiled=True)  38.3 us
    all_to_all x7, starting transfers between devices, body(): lax.all_to_all(shaped, 'tok', split_axis=0, concat_axis=0, tiled=True)  23 us
    unnamed x2, blocking collectives  18.7 us
    dot_general x1, matrix products, body(): jnp.dot(piece, policy_head, preferred_element_type=jnp.float32)  9.63 us
    unnamed x22, local copies, waits for them, and re-layouts  7.34 us
    dot_general x1, matrix products, body(): jnp.dot(piece, reference_head, preferred_element_type=jnp.float32)  5.92 us
    all_to_all x7, local copies, waits for them, and re-layouts, body(): lax.all_to_all(shaped, 'tok', split_axis=0, concat_axis=0, tiled=True)  4.75 us
  transfers between devices with their start and end apart: 8, of which 8 were waited for; matrix products, arithmetic and copies ran while one was open for 2% of the time, Pallas kernels for 0%

commit v1 on v0

--- a/solution.py
+++ b/solution.py
@@ -80,7 +80,21 @@
     vocab_count = lax.axis_size("vocab")
     tok_rows = hidden.shape[0]
     vocab_cols = policy_head.shape[1]
-    piece = lax.all_gather(hidden, "tok", axis=0, tiled=True)
+    ways, here, step_2 = (lax.axis_size("tok"), lax.axis_index("tok"), hidden.shape[0])
+    shape = [n * ways if d == 0 else n for d, n in enumerate(hidden.shape)]
+    full = lax.dynamic_update_slice_in_dim(
+        jnp.zeros(shape, hidden.dtype), hidden, here * step_2, axis=0
+    )
+    going_up = going_down = hidden
+    for far in range(1, ways // 2 + 1):
+        going_up = lax.ppermute(going_up, "tok", [(d, (d + 1) % ways) for d in range(ways)])
+        full = lax.dynamic_update_slice_in_dim(full, going_up, (here - far) % ways * step_2, axis=0)
+        if 2 * far < ways:
+            going_down = lax.ppermute(going_down, "tok", [(d, (d - 1) % ways) for d in range(ways)])
+            full = lax.dynamic_update_slice_in_dim(
+                full, going_down, (here + far) % ways * step_2, axis=0
+            )
+    piece = full
     summed = jnp.concatenate(
         [
             jnp.dot(piece, policy_head, preferred_element_type=jnp.float32),

time: 180 us -> 176 us (0.978)
  waiting for transfers between devices: 92.7 us -> 66.3 us
  starting transfers between devices: 23.1 us -> 49 us
  between operations: 15.5 us -> 2.33 us
  blocking collectives: 18.7 us -> 28.3 us
  matrix products: 15.6 us -> 12.8 us
  local copies, waits for them, and re-layouts: 12.7 us -> 14.7 us
    all_gather x1 -> x0, waiting for transfers between devices: 53.8 us -> none  [body(): piece = lax.all_gather(hidden, 'tok', axis=0, tiled=True)]
    ppermute x0 -> x7, waiting for transfers between devices: none -> 28 us  [the longest x4 18.8 us: body(): lax.ppermute(going_up, 'tok', [(d, (d + 1) % ways) for d in range(ways)])]
    ppermute x0 -> x7, starting transfers between devices: none -> 24.9 us  [the longest x3 16.3 us: body(): lax.ppermute(going_down, 'tok', [(d, (d - 1) % ways) for d in range(ways)])]
    unnamed x2, blocking collectives: 18.7 us -> 28.3 us
    dynamic_update_slice x0 -> x8, local copies, waits for them, and re-layouts: none -> 2.3 us  [the longest x4 1.15 us: body(): lax.dynamic_update_slice_in_dim(full, going_up, (here - far) % ways * ste...]
    unnamed x22 -> x36, local copies, waits for them, and re-layouts: 7.34 us -> 6.75 us
  transfers between devices with their start and end apart: 8 -> 14, of which waited for: 8 -> 10; matrix products, arithmetic and copies ran while one was open for 2% -> 3% of each run, Pallas kernels for 0% -> 0%
where the time goes in v1:
time: 176 us; the launch traced here: 175 us
  waiting for transfers between devices  66.3 us (38%)
  starting transfers between devices  49 us (28%)
  blocking collectives  28.3 us (16%)
  local copies, waits for them, and re-layouts  14.7 us (8%)
  matrix products  12.8 us (7%)
  between operations  2.33 us (1%)
    all_to_all x7, waiting for transfers between devices, body(): lax.all_to_all(shaped, 'tok', split_axis=0, concat_axis=0, tiled=True)  38.3 us
    unnamed x2, blocking collectives  28.3 us
    all_to_all x7, starting transfers between devices, body(): lax.all_to_all(shaped, 'tok', split_axis=0, concat_axis=0, tiled=True)  24.1 us
    ppermute x4, waiting for transfers between devices, body(): lax.ppermute(going_up, 'tok', [(d, (d + 1) % ways) for d in range(ways)])  18.8 us
    ppermute x3, starting transfers between devices, body(): lax.ppermute(going_down, 'tok', [(d, (d - 1) % ways) for d in range(ways)])  16.3 us
    ppermute x3, waiting for transfers between devices, body(): lax.ppermute(going_down, 'tok', [(d, (d - 1) % ways) for d in range(ways)])  9.17 us
    dot_general x1, matrix products, body(): jnp.dot(piece, policy_head, preferred_element_type=jnp.float32)  8.64 us
    ppermute x4, starting transfers between devices, body(): lax.ppermute(going_up, 'tok', [(d, (d + 1) % ways) for d in range(ways)])  8.58 us
  transfers between devices with their start and end apart: 14, of which 10 were waited for; matrix products, arithmetic and copies ran while one was open for 3% of the time, Pallas kernels for 0%

profile of v1, /device:TPU:0, one launch (start us, length us, event | category | flops | bytes accessed | tf_op | source)
XLA Modules:
  0.0 175.1 jit_solution(15850145136698909493)
XLA Ops:
  0.7 3.0 %collective-permute-start = (bf16[24,9216]{1,0:T(8,128)(2,1)}, bf16[24,9216]{1,0:T(8,128)(2,1)}, u32[]{:S(2)}, u32[]{:S(2)}) collective-permute-start(bf16[24,9216]{1,0:T(8,128)(2,1)} %param.6), channel_id=1, source_target_pairs={{0,4},{4,8},{8,12},{12,16},{16,20},{20,24},{24,28},{28,0},{1,5},{5... | collective-permute-start | bytes 1327112 | tf_op jit(solution)/shard_map/ppermute | solution.py:90
  3.7 3.1 %collective-permute-start.1 = (bf16[24,9216]{1,0:T(8,128)(2,1)}, bf16[24,9216]{1,0:T(8,128)(2,1)}, u32[]{:S(2)}, u32[]{:S(2)}) collective-permute-start(bf16[24,9216]{1,0:T(8,128)(2,1)} %param.6), channel_id=1, source_target_pairs={{0,28},{4,0},{8,4},{12,8},{16,12},{20,16},{24,20},{28,24},{1,29},{... | collective-permute-start | bytes 1327112 | tf_op jit(solution)/shard_map/ppermute | solution.py:93
  6.8 0.4 broadcast_in_dim.7
  7.2 0.7 copy-done
  8.0 0.6 dynamic-slice.5
  9.3 0.2 dynamic-update-slice.5
  9.5 22.6 %all-reduce.5 = s32[192]{0:T(256)S(1)} all-reduce(s32[192]{0:T(256)S(1)} %dynamic-update-slice.5), channel_id=1, replica_groups=mesh['tok'=8,'vocab'=4] {'tok'}, use_global_device_ids=true, to_apply=%add.5 | all-reduce | flops 192 | bytes 1536
  32.2 0.7 collective-permute-start.2
  32.9 4.1 %collective-permute-start.3 = (bf16[24,9216]{1,0:T(8,128)(2,1)}, bf16[24,9216]{1,0:T(8,128)(2,1)S(1)}, u32[]{:S(2)}, u32[]{:S(2)}) collective-permute-start(bf16[24,9216]{1,0:T(8,128)(2,1)} %collective-permute-done.1), channel_id=1, source_target_pairs={{0,28},{4,0},{8,4},{12,8},{16,12},{20,16},{24,20},{28,24},{1,29},{... | collective-permute-start | bytes 1327112 | tf_op jit(solution)/shard_map/ppermute | solution.py:93
  37.0 1.0 constant_dynamic-update-slice_fusion.6
  38.0 1.1 constant_dynamic-update-slice_fusion.5
  39.1 11.2 %collective-permute-done.2 = bf16[24,9216]{1,0:T(8,128)(2,1)S(1)} collective-permute-done((bf16[24,9216]{1,0:T(8,128)(2,1)}, bf16[24,9216]{1,0:T(8,128)(2,1)S(1)}, u32[]{:S(2)}, u32[]{:S(2)}) %collective-permute-start.2) | collective-permute-done | bytes 442400 | tf_op jit(solution)/shard_map/ppermute | solution.py:90
  50.2 2.4 %collective-permute-start.4 = (bf16[24,9216]{1,0:T(8,128)(2,1)S(1)}, bf16[24,9216]{1,0:T(8,128)(2,1)S(1)}, u32[]{:S(2)}, u32[]{:S(2)}) collective-permute-start(bf16[24,9216]{1,0:T(8,128)(2,1)S(1)} %collective-permute-done.2), channel_id=1, source_target_pairs={{0,4},{4,8},{8,12},{12,16},{16,20},{20,24},{24,28},{28,0},{1,5},{5... | collective-permute-start | bytes 1327112 | tf_op jit(solution)/shard_map/ppermute | solution.py:90
  52.6 9.1 %collective-permute-start.5 = (bf16[24,9216]{1,0:T(8,128)(2,1)S(1)}, bf16[24,9216]{1,0:T(8,128)(2,1)S(1)}, u32[]{:S(2)}, u32[]{:S(2)}) collective-permute-start(bf16[24,9216]{1,0:T(8,128)(2,1)S(1)} %collective-permute-done.3), channel_id=1, source_target_pairs={{0,28},{4,0},{8,4},{12,8},{16,12},{20,16},{24,20},{28,24},{1,29},{... | collective-permute-start | bytes 1327112 | tf_op jit(solution)/shard_map/ppermute | solution.py:93
  61.8 7.6 %collective-permute-done.4 = bf16[24,9216]{1,0:T(8,128)(2,1)S(1)} collective-permute-done((bf16[24,9216]{1,0:T(8,128)(2,1)S(1)}, bf16[24,9216]{1,0:T(8,128)(2,1)S(1)}, u32[]{:S(2)}, u32[]{:S(2)}) %collective-permute-start.4) | collective-permute-done | bytes 442400 | tf_op jit(solution)/shard_map/ppermute | solution.py:90
  69.4 2.5 %collective-permute-start.6 = (bf16[24,9216]{1,0:T(8,128)(2,1)S(1)}, bf16[24,9216]{1,0:T(8,128)(2,1)S(1)}, u32[]{:S(2)}, u32[]{:S(2)}) collective-permute-start(bf16[24,9216]{1,0:T(8,128)(2,1)S(1)} %collective-permute-done.4), channel_id=1, source_target_pairs={{0,4},{4,8},{8,12},{12,16},{16,20},{20,24},{24,28},{28,0},{1,5},{5... | collective-permute-start | bytes 1327112 | tf_op jit(solution)/shard_map/ppermute | solution.py:90
  72.0 9.2 %collective-permute-done.5 = bf16[24,9216]{1,0:T(8,128)(2,1)S(1)} collective-permute-done((bf16[24,9216]{1,0:T(8,128)(2,1)S(1)}, bf16[24,9216]{1,0:T(8,128)(2,1)S(1)}, u32[]{:S(2)}, u32[]{:S(2)}) %collective-permute-start.5) | collective-permute-done | bytes 442400 | tf_op jit(solution)/shard_map/ppermute | solution.py:93
  81.2 0.0 slice-start.1
  81.3 8.6 %fusion.24 = (f32[192]{0:T(256)S(1)}, f32[192,1024]{1,0:T(8,128)S(1)}) fusion(bf16[192,9216]{1,0:T(8,128)(2,1)S(1)} %constant_dynamic-update-slice_fusion, bf16[9216,1024]{1,0:T(8,128)(2,1)} %param.7), kind=kOutput, calls=%fused_computation.52 | convolution fusion | flops 3624075008 | bytes 23200512 | tf_op jit(solution)/shard_map/dot_general | solution.py:100
  89.9 0.1 slice-done.1
  90.0 1.2 slice-done.2
  91.2 1.2 slice-done.3
  92.4 0.6 slice-done.4
  93.0 4.2 %fusion.25 = (f32[192]{0:T(256)S(1)}, f32[192,1024]{1,0:T(8,128)S(1)}) fusion(bf16[192,9216]{1,0:T(8,128)(2,1)S(1)} %constant_dynamic-update-slice_fusion, bf16[9216,1024]{1,0:T(8,128)(2,1)S(1)} %bitcast.83), kind=kOutput, calls=%fused_computation.53 | convolution fusion | flops 3624075008 | bytes 23200512 | tf_op jit(solution)/shard_map/dot_general | solution.py:101
  97.2 0.7 multiply_reduce_fusion
  97.9 0.7 all_to_all.60
  98.6 4.3 %all-to-all-start.3 = ((f32[8,1,24]{2,1,0:T(1,128)}), f32[8,1,24]{2,1,0:T(1,128)S(1)}, u32[]{:S(2)}, u32[]{:S(2)}) async-start(f32[8,1,24]{2,1,0:T(1,128)} %all_to_all.60), calls=%async_computation.3 | async-start | bytes 8192 | tf_op jit(solution)/shard_map/all_to_all | solution.py:113
  102.9 0.7 all_to_all.54
  103.6 5.8 %all-to-all-done.3 = f32[8,1,24]{2,1,0:T(1,128)S(1)} async-done(((f32[8,1,24]{2,1,0:T(1,128)}), f32[8,1,24]{2,1,0:T(1,128)S(1)}, u32[]{:S(2)}, u32[]{:S(2)}) %all-to-all-start.3) | async-done | bytes 800 | tf_op jit(solution)/shard_map/all_to_all | solution.py:113
  109.4 3.3 %all-to-all-start.1 = ((f32[8,1,24]{2,1,0:T(1,128)}), f32[8,1,24]{2,1,0:T(1,128)S(1)}, u32[]{:S(2)}, u32[]{:S(2)}) async-start(f32[8,1,24]{2,1,0:T(1,128)} %all_to_all.54), calls=%async_computation.1 | async-start | bytes 8192 | tf_op jit(solution)/shard_map/all_to_all | solution.py:113
  112.8 0.7 all_to_all.64
  113.4 5.8 %all-to-all-done.1 = f32[8,1,24]{2,1,0:T(1,128)S(1)} async-done(((f32[8,1,24]{2,1,0:T(1,128)}), f32[8,1,24]{2,1,0:T(1,128)S(1)}, u32[]{:S(2)}, u32[]{:S(2)}) %all-to-all-start.1) | async-done | bytes 800 | tf_op jit(solution)/shard_map/all_to_all | solution.py:113
  119.2 3.3 %all-to-all-start.4 = ((f32[8,1,24]{2,1,0:T(1,128)}), f32[8,1,24]{2,1,0:T(1,128)S(1)}, u32[]{:S(2)}, u32[]{:S(2)}) async-start(f32[8,1,24]{2,1,0:T(1,128)} %all_to_all.64), calls=%async_computation.4 | async-start | bytes 8192 | tf_op jit(solution)/shard_map/all_to_all | solution.py:113
  122.5 0.7 all_to_all.52
  123.2 5.7 %all-to-all-done.4 = f32[8,1,24]{2,1,0:T(1,128)S(1)} async-done(((f32[8,1,24]{2,1,0:T(1,128)}), f32[8,1,24]{2,1,0:T(1,128)S(1)}, u32[]{:S(2)}, u32[]{:S(2)}) %all-to-all-start.4) | async-done | bytes 800 | tf_op jit(solution)/shard_map/all_to_all | solution.py:113
  128.9 3.2 %all-to-all-start = ((f32[8,1,24]{2,1,0:T(1,128)}), f32[8,1,24]{2,1,0:T(1,128)S(1)}, u32[]{:S(2)}, u32[]{:S(2)}) async-start(f32[8,1,24]{2,1,0:T(1,128)} %all_to_all.52), calls=%async_computation | async-start | bytes 8192 | tf_op jit(solution)/shard_map/all_to_all | solution.py:113
  132.2 0.7 all_to_all.56
  132.8 5.7 %all-to-all-done = f32[8,1,24]{2,1,0:T(1,128)S(1)} async-done(((f32[8,1,24]{2,1,0:T(1,128)}), f32[8,1,24]{2,1,0:T(1,128)S(1)}, u32[]{:S(2)}, u32[]{:S(2)}) %all-to-all-start) | async-done | bytes 800 | tf_op jit(solution)/shard_map/all_to_all | solution.py:113
  138.6 3.3 %all-to-all-start.2 = ((f32[8,1,24]{2,1,0:T(1,128)}), f32[8,1,24]{2,1,0:T(1,128)S(1)}, u32[]{:S(2)}, u32[]{:S(2)}) async-start(f32[8,1,24]{2,1,0:T(1,128)} %all_to_all.56), calls=%async_computation.2 | async-start | bytes 8192 | tf_op jit(solution)/shard_map/all_to_all | solution.py:113
  141.9 0.6 dynamic-slice
  143.2 0.7 all_to_all.67
  143.9 0.7 all_to_all.69
  144.6 3.8 %all-to-all-done.2 = f32[8,1,24]{2,1,0:T(1,128)S(1)} async-done(((f32[8,1,24]{2,1,0:T(1,128)}), f32[8,1,24]{2,1,0:T(1,128)S(1)}, u32[]{:S(2)}, u32[]{:S(2)}) %all-to-all-start.2) | async-done | bytes 800 | tf_op jit(solution)/shard_map/all_to_all | solution.py:113
  148.4 3.2 %all-to-all-start.5 = ((f32[8,1,24]{2,1,0:T(1,128)}), f32[8,1,24]{2,1,0:T(1,128)S(1)}, u32[]{:S(2)}, u32[]{:S(2)}) async-start(f32[8,1,24]{2,1,0:T(1,128)} %all_to_all.67), calls=%async_computation.5 | async-start | bytes 8192 | tf_op jit(solution)/shard_map/all_to_all | solution.py:113
  151.7 6.4 %all-to-all-done.5 = f32[8,1,24]{2,1,0:T(1,128)S(1)} async-done(((f32[8,1,24]{2,1,0:T(1,128)}), f32[8,1,24]{2,1,0:T(1,128)S(1)}, u32[]{:S(2)}, u32[]{:S(2)}) %all-to-all-start.5) | async-done | bytes 800 | tf_op jit(solution)/shard_map/all_to_all | solution.py:113
  158.0 3.3 %all-to-all-start.6 = ((f32[8,1,24]{2,1,0:T(1,128)}), f32[8,1,24]{2,1,0:T(1,128)S(1)}, u32[]{:S(2)}, u32[]{:S(2)}) async-start(f32[8,1,24]{2,1,0:T(1,128)} %all_to_all.69), calls=%async_computation.6 | async-start | bytes 8192 | tf_op jit(solution)/shard_map/all_to_all | solution.py:113
  161.4 0.2 dynamic-update-slice.1
  161.6 0.2 dynamic-update-slice
  161.8 0.2 dynamic-update-slice.3
  162.0 0.2 dynamic-update-slice.4
  162.2 0.2 dynamic-update-slice.2
  162.4 0.2 dynamic-update-slice.6
  162.7 5.1 %all-to-all-done.6 = f32[8,1,24]{2,1,0:T(1,128)S(1)} async-done(((f32[8,1,24]{2,1,0:T(1,128)}), f32[8,1,24]{2,1,0:T(1,128)S(1)}, u32[]{:S(2)}, u32[]{:S(2)}) %all-to-all-start.6) | async-done | bytes 800 | tf_op jit(solution)/shard_map/all_to_all | solution.py:113
  167.8 0.2 dynamic-update-slice.7
  168.0 5.6 %all-reduce.8 = (f32[96]{0:T(128)S(1)}, f32[96]{0:T(128)S(1)}, f32[96]{0:T(128)S(1)}, f32[96]{0:T(128)S(1)}, f32[96]{0:T(128)S(1)}, /*index=5*/f32[96]{0:T(128)S(1)}, f32[96]{0:T(128)S(1)}) all-reduce(f32[96]{0:T(128)S(1)} %dynamic-update-slice, f32[96]{0:T(128)S(1)} %dynamic-update-slice.1, ...), channel_id=2, replica_groups=mesh['tok'=8,'vocab'=4] {'vocab'}, use_global_device_ids=true, to_apply=%add | all-reduce | flops 672 | bytes 5376
  173.7 0.1 reshape.43
  173.7 0.1 reshape.44
  173.8 0.1 reshape.45
  173.9 0.1 reshape.46
  174.0 0.1 reshape.47
  174.1 0.1 reshape.48
  174.1 0.1 reshape.49
  174.2 0.3 while.27
  174.5 0.5 subtract_add_fusion
  (50 shorter events, 0.6 us)
Async XLA Ops:
  0.6 7.4 %copy-start.3 = (u32[32]{0:T(128)S(1)}, u32[32]{0:T(128)}, u32[]{:S(2)}) copy-start(u32[32]{0:T(128)} %constant.137) | copy-start | bytes 388
  0.6 8.6 %copy-start.1 = (s32[24]{0:T(128)S(1)}, s32[24]{0:T(128)}, u32[]{:S(2)}) copy-start(s32[24]{0:T(128)} %param.9) | copy-start | bytes 292
  0.7 31.5 %collective-permute-start = (bf16[24,9216]{1,0:T(8,128)(2,1)}, bf16[24,9216]{1,0:T(8,128)(2,1)}, u32[]{:S(2)}, u32[]{:S(2)}) collective-permute-start(bf16[24,9216]{1,0:T(8,128)(2,1)} %param.6), channel_id=1, source_target_pairs={{0,4},{4,8},{8,12},{12,16},{16,20},{20,24},{24,28},{28,0},{1,5},{5... | collective-permute-start | bytes 1327112 | tf_op jit(solution)/shard_map/ppermute | solution.py:90
  3.7 29.2 %collective-permute-start.1 = (bf16[24,9216]{1,0:T(8,128)(2,1)}, bf16[24,9216]{1,0:T(8,128)(2,1)}, u32[]{:S(2)}, u32[]{:S(2)}) collective-permute-start(bf16[24,9216]{1,0:T(8,128)(2,1)} %param.6), channel_id=1, source_target_pairs={{0,28},{4,0},{8,4},{12,8},{16,12},{20,16},{24,20},{28,24},{1,29},{... | collective-permute-start | bytes 1327112 | tf_op jit(solution)/shard_map/ppermute | solution.py:93
  6.8 1.0 copy-start
  32.2 18.0 %collective-permute-start.2 = (bf16[24,9216]{1,0:T(8,128)(2,1)}, bf16[24,9216]{1,0:T(8,128)(2,1)S(1)}, u32[]{:S(2)}, u32[]{:S(2)}) collective-permute-start(bf16[24,9216]{1,0:T(8,128)(2,1)} %collective-permute-done), channel_id=1, source_target_pairs={{0,4},{4,8},{8,12},{12,16},{16,20},{20,24},{24,28},{28,0},{1,5},{5... | collective-permute-start | bytes 1327112 | tf_op jit(solution)/shard_map/ppermute | solution.py:90
  32.9 19.7 %collective-permute-start.3 = (bf16[24,9216]{1,0:T(8,128)(2,1)}, bf16[24,9216]{1,0:T(8,128)(2,1)S(1)}, u32[]{:S(2)}, u32[]{:S(2)}) collective-permute-start(bf16[24,9216]{1,0:T(8,128)(2,1)} %collective-permute-done.1), channel_id=1, source_target_pairs={{0,28},{4,0},{8,4},{12,8},{16,12},{20,16},{24,20},{28,24},{1,29},{... | collective-permute-start | bytes 1327112 | tf_op jit(solution)/shard_map/ppermute | solution.py:93
  50.2 19.2 %collective-permute-start.4 = (bf16[24,9216]{1,0:T(8,128)(2,1)S(1)}, bf16[24,9216]{1,0:T(8,128)(2,1)S(1)}, u32[]{:S(2)}, u32[]{:S(2)}) collective-permute-start(bf16[24,9216]{1,0:T(8,128)(2,1)S(1)} %collective-permute-done.2), channel_id=1, source_target_pairs={{0,4},{4,8},{8,12},{12,16},{16,20},{20,24},{24,28},{28,0},{1,5},{5... | collective-permute-start | bytes 1327112 | tf_op jit(solution)/shard_map/ppermute | solution.py:90
  52.6 28.5 %collective-permute-start.5 = (bf16[24,9216]{1,0:T(8,128)(2,1)S(1)}, bf16[24,9216]{1,0:T(8,128)(2,1)S(1)}, u32[]{:S(2)}, u32[]{:S(2)}) collective-permute-start(bf16[24,9216]{1,0:T(8,128)(2,1)S(1)} %collective-permute-done.3), channel_id=1, source_target_pairs={{0,28},{4,0},{8,4},{12,8},{16,12},{20,16},{24,20},{28,24},{1,29},{... | collective-permute-start | bytes 1327112 | tf_op jit(solution)/shard_map/ppermute | solution.py:93
  69.4 11.7 %collective-permute-start.6 = (bf16[24,9216]{1,0:T(8,128)(2,1)S(1)}, bf16[24,9216]{1,0:T(8,128)(2,1)S(1)}, u32[]{:S(2)}, u32[]{:S(2)}) collective-permute-start(bf16[24,9216]{1,0:T(8,128)(2,1)S(1)} %collective-permute-done.4), channel_id=1, source_target_pairs={{0,4},{4,8},{8,12},{12,16},{16,20},{20,24},{24,28},{28,0},{1,5},{5... | collective-permute-start | bytes 1327112 | tf_op jit(solution)/shard_map/ppermute | solution.py:90
  81.2 8.7 %slice-start = ((s8[18874368]{0:T(1024)(128)(4,1)}), s8[4194304]{0:T(1024)(128)(4,1)S(1)}, s32[]{:S(2)}) async-start(s8[18874368]{0:T(1024)(128)(4,1)} %bitcast.82), calls=%async_computation.7 | async-start | bytes 8388608
  81.2 8.8 %slice-start.1 = ((s8[18874368]{0:T(1024)(128)(4,1)}), s8[4194304]{0:T(1024)(128)(4,1)S(1)}, s32[]{:S(2)}) async-start(s8[18874368]{0:T(1024)(128)(4,1)} %bitcast.82), calls=%async_computation.8 | async-start | bytes 8388608
  81.2 10.0 %slice-start.2 = ((s8[18874368]{0:T(1024)(128)(4,1)}), s8[4194304]{0:T(1024)(128)(4,1)S(1)}, s32[]{:S(2)}) async-start(s8[18874368]{0:T(1024)(128)(4,1)} %bitcast.82), calls=%async_computation.9 | async-start | bytes 8388608
  81.3 11.2 %slice-start.3 = ((s8[18874368]{0:T(1024)(128)(4,1)}), s8[4194304]{0:T(1024)(128)(4,1)S(1)}, s32[]{:S(2)}) async-start(s8[18874368]{0:T(1024)(128)(4,1)} %bitcast.82), calls=%async_computation.10 | async-start | bytes 8388608
  81.3 11.8 %slice-start.4 = ((s8[18874368]{0:T(1024)(128)(4,1)}), s8[2097152]{0:T(1024)(128)(4,1)S(1)}, s32[]{:S(2)}) async-start(s8[18874368]{0:T(1024)(128)(4,1)} %bitcast.82), calls=%async_computation.11 | async-start | bytes 4194304
  93.0 48.9 %copy-start.2 = (u32[32]{0:T(128)S(1)}, u32[32]{0:T(128)}, u32[]{:S(2)}) copy-start(u32[32]{0:T(128)} %constant.112) | copy-start | bytes 388
  98.6 10.8 %all-to-all-start.3 = ((f32[8,1,24]{2,1,0:T(1,128)}), f32[8,1,24]{2,1,0:T(1,128)S(1)}, u32[]{:S(2)}, u32[]{:S(2)}) async-start(f32[8,1,24]{2,1,0:T(1,128)} %all_to_all.60), calls=%async_computation.3 | async-start | bytes 8192 | tf_op jit(solution)/shard_map/all_to_all | solution.py:113
  109.4 9.8 %all-to-all-start.1 = ((f32[8,1,24]{2,1,0:T(1,128)}), f32[8,1,24]{2,1,0:T(1,128)S(1)}, u32[]{:S(2)}, u32[]{:S(2)}) async-start(f32[8,1,24]{2,1,0:T(1,128)} %all_to_all.54), calls=%async_computation.1 | async-start | bytes 8192 | tf_op jit(solution)/shard_map/all_to_all | solution.py:113
  119.2 9.7 %all-to-all-start.4 = ((f32[8,1,24]{2,1,0:T(1,128)}), f32[8,1,24]{2,1,0:T(1,128)S(1)}, u32[]{:S(2)}, u32[]{:S(2)}) async-start(f32[8,1,24]{2,1,0:T(1,128)} %all_to_all.64), calls=%async_computation.4 | async-start | bytes 8192 | tf_op jit(solution)/shard_map/all_to_all | solution.py:113
  128.9 9.7 %all-to-all-start = ((f32[8,1,24]{2,1,0:T(1,128)}), f32[8,1,24]{2,1,0:T(1,128)S(1)}, u32[]{:S(2)}, u32[]{:S(2)}) async-start(f32[8,1,24]{2,1,0:T(1,128)} %all_to_all.52), calls=%async_computation | async-start | bytes 8192 | tf_op jit(solution)/shard_map/all_to_all | solution.py:113
  138.6 9.8 %all-to-all-start.2 = ((f32[8,1,24]{2,1,0:T(1,128)}), f32[8,1,24]{2,1,0:T(1,128)S(1)}, u32[]{:S(2)}, u32[]{:S(2)}) async-start(f32[8,1,24]{2,1,0:T(1,128)} %all_to_all.56), calls=%async_computation.2 | async-start | bytes 8192 | tf_op jit(solution)/shard_map/all_to_all | solution.py:113
  148.4 9.7 %all-to-all-start.5 = ((f32[8,1,24]{2,1,0:T(1,128)}), f32[8,1,24]{2,1,0:T(1,128)S(1)}, u32[]{:S(2)}, u32[]{:S(2)}) async-start(f32[8,1,24]{2,1,0:T(1,128)} %all_to_all.67), calls=%async_computation.5 | async-start | bytes 8192 | tf_op jit(solution)/shard_map/all_to_all | solution.py:113
  158.0 9.7 %all-to-all-start.6 = ((f32[8,1,24]{2,1,0:T(1,128)}), f32[8,1,24]{2,1,0:T(1,128)S(1)}, u32[]{:S(2)}, u32[]{:S(2)}) async-start(f32[8,1,24]{2,1,0:T(1,128)} %all_to_all.69), calls=%async_computation.6 | async-start | bytes 8192 | tf_op jit(solution)/shard_map/all_to_all | solution.py:113
